TPU v7x, 32 devices: a whole 2x2x4 slice. The times are simulated.
32 devices in a mesh: fsdp: 2 (over x), context: 4 (over z), tensor: 4 (over y, core).
Axes of the slice: x: 2, y: 2, z: 4, core: 2. Of those that a mesh axis runs over, the one named last changes fastest.
Arguments:
- activations: bfloat16 [2, 2048, 1152], P('fsdp', 'context'), may hold values from -6 to 6
- positions: int32 [2, 2048], P('fsdp', 'context'), may hold values from 0 to 2047, as said below
- seg_ids: int32 [2, 2048], P('fsdp', 'context'), may hold values from 0 to 3, as said below
- norm_gains: bfloat16 [4, 1152], P(None, ('fsdp', 'context')), may hold values from 0.5 to 1.5
- head_gains: bfloat16 [2, 256], P(None, ('fsdp', 'context')), may hold values from 0.25 to 1.75
- w_query: bfloat16 [1152, 1024], P(('fsdp', 'context'), 'tensor'), may hold values from -0.1875 to 0.1875
- w_keyval: bfloat16 [1152, 512], P(('fsdp', 'context')), may hold values from -0.1875 to 0.1875
- w_out: bfloat16 [1152, 1024], P(('fsdp', 'context'), 'tensor'), may hold values from -0.1875 to 0.1875
- w_gateup: bfloat16 [1152, 2, 6912], P(('fsdp', 'context'), None, 'tensor'), may hold values from -0.1875 to 0.1875
- w_down: bfloat16 [1152, 6912], P(('fsdp', 'context'), 'tensor'), may hold values from -0.078125 to 0.078125
- cotangent: bfloat16 [2, 2048, 1152], P('fsdp', 'context'), may hold values from -6 to 6
Outputs:
- block_output: bfloat16 [2, 2048, 1152], P('fsdp', 'context')
- input_grad: bfloat16 [2, 2048, 1152], P('fsdp', 'context')
- norm_gains_grad: float32 [4, 1152], P(None, ('fsdp', 'context'))
- head_gains_grad: float32 [2, 256], P(None, ('fsdp', 'context'))
- w_query_grad: float32 [1152, 1024], P(('fsdp', 'context'), 'tensor')
- w_keyval_grad: float32 [1152, 512], P(('fsdp', 'context'))
- w_out_grad: float32 [1152, 1024], P(('fsdp', 'context'), 'tensor')
- w_gateup_grad: float32 [1152, 2, 6912], P(('fsdp', 'context'), None, 'tensor')
- w_down_grad: float32 [1152, 6912], P(('fsdp', 'context'), 'tensor')
Inputs may be any that keep to these rules, and one draw needn't show every extreme that they name: `positions`: within a sequence, a document is a run of consecutive tokens with one document number; numbers never fall along a sequence. Positions are 0 at a document's first token and rise by one from token to token inside it. The first sequence is one document. `seg_ids`: document numbers of a sequence start at 0 and never fall along it.
All inputs are finite; a program needn't handle non-finite values.
Results may differ from a plain program's by a relative error of at most 0.024.
Values may be sent and summed in bfloat16 or wider, within the bound.
A program may use at most 192 MiB of HBM per device.

v0:
```python
import jax
import jax.numpy as jnp
from jax import lax
from jax.sharding import PartitionSpec as P

HD = 256
WINDOW = 512
EPSILON = 1e-06


def from_behind(block, axis, distance):
    devices = range(lax.axis_size(axis))
    route = [(i - distance, i) for i in devices if i - distance in devices]
    return lax.ppermute(block, axis, route)


def rms_norm(values, gain):
    factor = lax.rsqrt(jnp.mean(values * values, axis=-1, keepdims=True) + EPSILON)
    return values * factor * gain


def rotate(tensor, places):
    width_all = tensor.shape[-1]
    half_width = width_all // 2
    freqs = jnp.power(10000.0, -jnp.arange(half_width, dtype=jnp.float32) * 2.0 / width_all)
    angles = places.astype(jnp.float32)[:, None] * freqs[None, :]
    cosine = jnp.cos(angles)[:, None, :]
    sine = jnp.sin(angles)[:, None, :]
    first_half = tensor[..., :half_width]
    second_half = tensor[..., half_width:]
    return jnp.concatenate(
        [first_half * cosine - second_half * sine, second_half * cosine + first_half * sine],
        axis=-1,
    )


def glu(gate_up):
    return jax.nn.gelu(gate_up[:, 0], approximate=True) * gate_up[:, 1]


def contract_last(left_side, right_side):
    return lax.dot_general(
        left_side, right_side, (((1,), (1,)), ((), ())), preferred_element_type=jnp.float32
    )


def contract_first(left_side, right_side):
    return lax.dot_general(
        left_side, right_side, (((0,), (0,)), ((), ())), preferred_element_type=jnp.float32
    )


def shards(
    activations,
    positions,
    seg_ids,
    norm_gains,
    head_gains,
    w_query,
    w_keyval,
    w_out,
    w_gateup,
    w_down,
    cotangent,
):
    tokens = activations.shape[1]
    local_heads = w_query.shape[1] // HD
    inputs = activations[0].astype(jnp.float32)
    places = positions[0]
    documents = seg_ids[0]
    gains_all, heads_all, query_all, keyval_all, out_all = (
        lax.all_gather(norm_gains, ("fsdp", "context"), axis=1, tiled=True),
        lax.all_gather(head_gains, ("fsdp", "context"), axis=1, tiled=True),
        lax.all_gather(w_query, ("fsdp", "context"), axis=0, tiled=True),
        lax.all_gather(w_keyval, ("fsdp", "context"), axis=0, tiled=True),
        lax.all_gather(w_out, ("fsdp", "context"), axis=0, tiled=True),
    )
    gains_f = gains_all.astype(jnp.float32)
    heads_f = heads_all.astype(jnp.float32)
    normed_f, input_back = jax.vjp(rms_norm, inputs, gains_f[0])
    normed = normed_f.astype(jnp.bfloat16)
    query_raw = jnp.dot(normed, query_all, preferred_element_type=jnp.float32).reshape(
        tokens, local_heads, HD
    )
    keyval_raw = jnp.dot(normed, keyval_all, preferred_element_type=jnp.float32)

    def prepare(raw_heads, head_gain):
        return rotate(rms_norm(raw_heads, head_gain), places)

    query_rot, query_back = jax.vjp(prepare, query_raw, heads_f[0])
    key_rot, key_back = jax.vjp(prepare, keyval_raw[:, None, :HD], heads_f[1])
    queries = query_rot.astype(jnp.bfloat16)
    own_keyval = jnp.concatenate([key_rot[:, 0], keyval_raw[:, HD:]], axis=1).astype(jnp.bfloat16)
    labels = jnp.stack([places, documents])
    keep_from = tokens - tokens
    left_keyval, left_labels = from_behind((own_keyval, labels), "context", 1)
    keys_all = jnp.concatenate([left_keyval, own_keyval], axis=0)
    key_places = jnp.concatenate([left_labels[0], places])
    key_documents = jnp.concatenate([left_labels[1], documents])
    has_left = lax.axis_index("context") > 0
    key_live = jnp.concatenate([jnp.full((tokens,), has_left), jnp.ones((tokens,), dtype=bool)])
    scale_factor = HD ** (-0.5)
    block_rows = 512
    block_starts = jnp.arange(tokens // block_rows) * block_rows

    def block_scores():
        spacing = places[:, None] - key_places[None, :]
        visible = (
            key_live[None, :]
            & (documents[:, None] == key_documents[None, :])
            & (spacing >= 0)
            & (spacing < WINDOW)
        )
        raw_scores = (
            jnp.einsum("qhd,kd->hqk", queries, keys_all[:, :HD], preferred_element_type=jnp.float32)
            * scale_factor
        )
        return (jnp.where(visible[None], raw_scores, -1e30), keys_all, queries)

    def forward_block(start):
        scores, near_keyval, query_block = block_scores()
        row_top = jnp.max(scores, axis=-1, keepdims=True)
        raised = jnp.exp(scores - row_top)
        row_total = jnp.sum(raised, axis=-1, keepdims=True)
        probs = raised / row_total
        mixed_block = jnp.einsum(
            "hqk,kd->qhd",
            probs.astype(jnp.bfloat16),
            near_keyval[:, HD:],
            preferred_element_type=jnp.float32,
        )
        return (mixed_block.astype(jnp.bfloat16), row_top + jnp.log(row_total))

    mixed_blocks, log_blocks = lax.map(forward_block, block_starts)
    mixed_low = mixed_blocks.reshape(tokens, local_heads * HD)
    branch = lax.psum(contract_last(mixed_low, out_all).astype(jnp.bfloat16), "tensor").astype(
        jnp.float32
    )
    post_attn, post_attn_back = jax.vjp(rms_norm, branch, gains_f[1])
    hidden = inputs + post_attn
    normed_mlp_f, pre_mlp_back = jax.vjp(rms_norm, hidden, gains_f[2])
    normed_mlp = normed_mlp_f.astype(jnp.bfloat16)
    columns = normed_mlp
    gate_up = jnp.einsum(
        "bn,nkf->bkf",
        columns,
        lax.all_gather(w_gateup, ("fsdp", "context"), axis=0, tiled=True),
        preferred_element_type=jnp.float32,
    )
    active_f, glu_back = jax.vjp(glu, gate_up)
    active = active_f.astype(jnp.bfloat16)
    down = lax.psum(
        contract_last(
            active, lax.all_gather(w_down, ("fsdp", "context"), axis=0, tiled=True)
        ).astype(jnp.bfloat16),
        "tensor",
    ).astype(jnp.float32)
    post_mlp, post_mlp_back = jax.vjp(rms_norm, down, gains_f[3])
    result = hidden + post_mlp
    grad_out = cotangent[0].astype(jnp.float32)
    d_down, gain_post_mlp = post_mlp_back(grad_out)
    down_low = d_down.astype(jnp.bfloat16)
    columns = down_low
    d_active = jnp.dot(
        columns,
        lax.all_gather(w_down, ("fsdp", "context"), axis=0, tiled=True),
        preferred_element_type=jnp.float32,
    )
    d_gate_up = glu_back(d_active)[0].astype(jnp.bfloat16)
    d_normed_part = jnp.einsum(
        "bkf,nkf->bn",
        d_gate_up,
        lax.all_gather(w_gateup, ("fsdp", "context"), axis=0, tiled=True),
        preferred_element_type=jnp.float32,
    )
    d_normed_mlp = lax.psum(d_normed_part.astype(jnp.bfloat16), "tensor").astype(jnp.float32)
    d_hidden_norm, gain_pre_mlp = pre_mlp_back(d_normed_mlp)
    d_hidden = grad_out + d_hidden_norm
    features = normed_mlp
    grad_cols = down_low
    gate_up_term = jnp.einsum(
        "bn,bkf->nkf", features, d_gate_up, preferred_element_type=jnp.float32
    )
    down_term = contract_first(grad_cols, active)
    scatter = lambda part: lax.psum_scatter(
        part.astype(jnp.bfloat16), ("fsdp", "context"), scatter_dimension=0, tiled=True
    ).astype(jnp.float32)
    gate_grad = scatter(gate_up_term[:, 0])
    up_grad = scatter(gate_up_term[:, 1])
    down_grad = scatter(down_term)
    d_branch, gain_post_attn = post_attn_back(d_hidden)
    branch_low = d_branch.astype(jnp.bfloat16)
    d_mixed = jnp.dot(branch_low, out_all, preferred_element_type=jnp.float32)
    d_mixed_low = d_mixed.astype(jnp.bfloat16).reshape(tokens, local_heads, HD)

    def backward_block(carry, item):
        start, log_block = item
        scores, near_keyval, query_block = block_scores()
        probs_again = jnp.exp(scores - log_block)
        d_probs = jnp.einsum(
            "qhd,kd->hqk", d_mixed_low, near_keyval[:, HD:], preferred_element_type=jnp.float32
        )
        row_inner = jnp.sum(probs_again * d_probs, axis=-1, keepdims=True)
        d_scores = (probs_again * (d_probs - row_inner)).astype(jnp.bfloat16)
        d_query_block = (
            jnp.einsum(
                "hqk,kd->qhd", d_scores, near_keyval[:, :HD], preferred_element_type=jnp.float32
            )
            * scale_factor
        )
        d_keys = (
            jnp.einsum("hqk,qhd->kd", d_scores, query_block, preferred_element_type=jnp.float32)
            * scale_factor
        )
        d_values = jnp.einsum(
            "hqk,qhd->kd",
            probs_again.astype(jnp.bfloat16),
            d_mixed_low,
            preferred_element_type=jnp.float32,
        )
        updated = carry + jnp.concatenate([d_keys, d_values], axis=1)
        return (updated, d_query_block)

    d_keyval, d_query_blocks = lax.scan(
        backward_block,
        jnp.zeros((tokens + tokens, 2 * HD), jnp.float32),
        (block_starts, log_blocks),
    )
    d_queries = d_query_blocks.reshape(tokens, local_heads, HD)
    returned = from_behind(d_keyval[:tokens].astype(jnp.bfloat16), "context", -1).astype(
        jnp.float32
    )
    own_grad = d_keyval[tokens:].at[keep_from:].add(returned)
    d_query_raw, gain_query = query_back(d_queries)
    d_query_low = d_query_raw.reshape(tokens, local_heads * HD).astype(jnp.bfloat16)
    d_normed_query, keyval_grad, gain_query_all = (
        lax.psum(contract_last(d_query_low, query_all).astype(jnp.bfloat16), "tensor").astype(
            jnp.float32
        ),
        lax.psum(own_grad.astype(jnp.bfloat16), "tensor").astype(jnp.float32),
        lax.psum(gain_query.astype(jnp.bfloat16), "tensor").astype(jnp.float32),
    )
    d_key_raw, gain_key = key_back(keyval_grad[:, None, :HD])
    d_keyval_low = jnp.concatenate([d_key_raw[:, 0], keyval_grad[:, HD:]], axis=1).astype(
        jnp.bfloat16
    )
    d_normed = d_normed_query + contract_last(d_keyval_low, keyval_all)
    d_input_norm, gain_input = input_back(d_normed)
    input_total = d_hidden + d_input_norm
    features = normed
    grad_cols = branch_low
    attn_grads = lax.psum_scatter(
        jnp.stack(
            [contract_first(features, d_query_low), contract_first(grad_cols, mixed_low)], axis=1
        ).astype(jnp.bfloat16),
        ("fsdp", "context"),
        scatter_dimension=0,
        tiled=True,
    ).astype(jnp.float32)
    keyval_term = contract_first(normed, d_keyval_low)
    gain_terms = jnp.stack([gain_input, gain_post_attn, gain_pre_mlp, gain_post_mlp])
    head_terms = jnp.stack([gain_query_all, gain_key])
    gain_grad, head_grad, keyval_weight_grad = (
        lax.psum_scatter(
            gain_terms.astype(jnp.bfloat16), ("fsdp", "context"), scatter_dimension=1, tiled=True
        ).astype(jnp.float32),
        lax.psum_scatter(
            head_terms.astype(jnp.bfloat16), ("fsdp", "context"), scatter_dimension=1, tiled=True
        ).astype(jnp.float32),
        lax.psum_scatter(
            keyval_term.astype(jnp.bfloat16), ("fsdp", "context"), scatter_dimension=0, tiled=True
        ).astype(jnp.float32),
    )
    return (
        result[None].astype(jnp.bfloat16),
        input_total[None].astype(jnp.bfloat16),
        gain_grad,
        head_grad,
        attn_grads[:, 0],
        keyval_weight_grad,
        attn_grads[:, 1],
        jnp.stack([gate_grad, up_grad], axis=1),
        down_grad,
    )


def solution(mesh):
    return jax.shard_map(
        shards,
        mesh=mesh,
        in_specs=(
            P("fsdp", "context", None),
            P("fsdp", "context"),
            P("fsdp", "context"),
            P(None, ("fsdp", "context")),
            P(None, ("fsdp", "context")),
            P(("fsdp", "context"), "tensor"),
            P(("fsdp", "context"), None),
            P(("fsdp", "context"), "tensor"),
            P(("fsdp", "context"), None, "tensor"),
            P(("fsdp", "context"), "tensor"),
            P("fsdp", "context", None),
        ),
        out_specs=(
            P("fsdp", "context", None),
            P("fsdp", "context", None),
            P(None, ("fsdp", "context")),
            P(None, ("fsdp", "context")),
            P(("fsdp", "context"), "tensor"),
            P(("fsdp", "context"), None),
            P(("fsdp", "context"), "tensor"),
            P(("fsdp", "context"), None, "tensor"),
            P(("fsdp", "context"), "tensor"),
        ),
        check_vma=False,
    )
```

profile of v0, /device:TPU:0, one launch (start us, length us, event | category | flops | bytes accessed | tf_op | source)
XLA Modules:
  0.0 1111.7 jit_solution(1959116816128827641)
XLA Ops:
  8.7 4.9 collective-permute-start.1
  14.3 18.8 %all-gather.1 = bf16[8,32,2]{1,2,0:T(2,128)(2,1)S(1)} all-gather(bf16[1,32,2]{1,2,0:T(2,128)(2,1)} %bitcast.266), channel_id=1, replica_groups=mesh['fsdp'=2,'context'=4,'tensor'=4] {'fsdp','context'}, dimensions={0}, use_global_device_ids=true | all-gather | bytes 1152 | tf_op jit(solution)/shard_map/all_gather | solution.py:73
  33.2 27.2 %all-gather = bf16[8,144,4]{1,2,0:T(4,128)(2,1)S(1)} all-gather(bf16[1,144,4]{1,2,0:T(4,128)(2,1)} %bitcast.265), channel_id=1, replica_groups=mesh['fsdp'=2,'context'=4,'tensor'=4] {'fsdp','context'}, dimensions={0}, use_global_device_ids=true | all-gather | bytes 10368 | tf_op jit(solution)/shard_map/all_gather | solution.py:72
  62.8 32.5 %all_gather.26 = bf16[1152,256]{1,0:T(8,128)(2,1)S(1)} all-gather(bf16[144,256]{1,0:T(8,128)(2,1)} %param.20), channel_id=1, replica_groups=mesh['fsdp'=2,'context'=4,'tensor'=4] {'fsdp','context'}, dimensions={0}, use_global_device_ids=true | all-gather | bytes 663552 | tf_op jit(solution)/shard_map/all_gather | solution.py:74
  104.4 33.8 %all_gather.27 = bf16[1152,256]{1,0:T(8,128)(2,1)S(1)} all-gather(bf16[144,256]{1,0:T(8,128)(2,1)S(1)} %copy-done.32), channel_id=1, replica_groups=mesh['fsdp'=2,'context'=4,'tensor'=4] {'fsdp','context'}, dimensions={0}, use_global_device_ids=true | all-gather | bytes 663552 | tf_op jit(solution)/shard_map/all_gather | solution.py:76
  146.2 36.1 %all-reduce.13.cloned.1.call-done = bf16[512,1152]{1,0:T(8,128)(2,1)} async-done(((bf16[512,1152]{1,0:T(8,128)(2,1)}), bf16[512,1152]{1,0:T(8,128)(2,1)}) %all-reduce.13.cloned.1.call-update) | async-done | bytes 1179664 | tf_op jit(solution)/shard_map/psum | solution.py:136
  188.6 119.4 %all-gather.8.cloned.1.call-done = bf16[1152,2,1728]{2,0,1:T(8,128)(2,1)} async-done(((bf16[144,2,1728]{2,0,1:T(8,128)(2,1)}), bf16[1152,2,1728]{2,0,1:T(8,128)(2,1)}) %all-gather.8.cloned.1.call-update) | async-done | bytes 7962640 | tf_op jit(solution)/shard_map/all_gather | solution.py:147
  308.0 8.2 fusion.114
  321.5 58.5 %all-gather.10.cloned.1.call-done = bf16[1152,1728]{1,0:T(8,128)(2,1)} async-done(((bf16[144,1728]{1,0:T(8,128)(2,1)}), bf16[1152,1728]{1,0:T(8,128)(2,1)}) %all-gather.10.cloned.1.call-update) | async-done | bytes 3981328 | tf_op jit(solution)/shard_map/all_gather | solution.py:154
  380.0 6.3 convolution_convert_fusion.4
  386.6 36.0 %all-reduce.15.cloned.1.call-done = bf16[512,1152]{1,0:T(8,128)(2,1)} async-done(((bf16[512,1152]{1,0:T(8,128)(2,1)}), bf16[512,1152]{1,0:T(8,128)(2,1)}) %all-reduce.15.cloned.1.call-update) | async-done | bytes 1179664 | tf_op jit(solution)/shard_map/psum | solution.py:152
  427.9 10.7 multiply_bitcast_fusion
  440.3 8.1 fusion.7
  450.2 36.1 %all-reduce.17.cloned.1.call-done = bf16[512,1152]{1,0:T(8,128)(2,1)} async-done(((bf16[512,1152]{1,0:T(8,128)(2,1)}), bf16[512,1152]{1,0:T(8,128)(2,1)}) %all-reduce.17.cloned.1.call-update) | async-done | bytes 1179664 | tf_op jit(solution)/shard_map/psum | solution.py:176
  486.4 3.6 fusion.29
  490.1 5.1 fusion.25
  505.7 11.6 %collective-permute-done.2 = bf16[512,512]{0,1:T(8,128)(2,1)S(1)} collective-permute-done((bf16[512,512]{0,1:T(8,128)(2,1)S(1)}, bf16[512,512]{0,1:T(8,128)(2,1)S(1)}, u32[]{:S(2)}, u32[]{:S(2)}) %collective-permute-start.2) | collective-permute-done | bytes 524320 | tf_op jit(solution)/shard_map/ppermute | solution.py:14
  523.5 7.2 psum.47
  535.6 27.2 %all-reduce.19.cloned.1.call-done = (bf16[512,1152]{1,0:T(8,128)(2,1)}, bf16[512,512]{0,1:T(8,128)(2,1)}) async-done(((bf16[512,1152]{1,0:T(8,128)(2,1)}, bf16[512,512]{0,1:T(8,128)(2,1)}), (bf16[512,1152]{1,0:T(8,128)(2,1)}, bf16[512,512]{0,1:T(8,128)(2,1)})) %all-reduce.19.cloned.1.call-update) | async-done | bytes 1703952 | tf_op jit(solution)/shard_map/psum | solution.py:237
  579.3 9.3 convolution_convert_fusion
  588.6 3.5 slice_bitcast_fusion.1
  592.1 6.5 copy.38
  598.6 6.5 copy.40
  606.8 6.3 convolution_convert_fusion.1
  613.8 4.0 fusion.52
  617.8 16.4 %reduce-scatter.24.cloned.1.call-done = bf16[32,2]{1,0:T(8,128)(2,1)} async-done(((bf16[256,2]{1,0:T(8,128)(2,1)}), bf16[32,2]{1,0:T(8,128)(2,1)}) %reduce-scatter.24.cloned.1.call-update) | async-done | bytes 144
  635.6 60.7 %reduce-scatter.22.cloned.1.call-done = bf16[144,4]{1,0:T(8,128)(2,1)} async-done(((bf16[1152,4]{1,0:T(8,128)(2,1)}), bf16[144,4]{1,0:T(8,128)(2,1)}) %reduce-scatter.22.cloned.1.call-update) | async-done | bytes 1168
  697.8 65.6 %reduce-scatter.16.cloned.1.call-done = bf16[144,2,256]{2,0,1:T(8,128)(2,1)} async-done(((bf16[1152,2,256]{2,0,1:T(8,128)(2,1)}), bf16[144,2,256]{2,0,1:T(8,128)(2,1)}) %reduce-scatter.16.cloned.1.call-update) | async-done | bytes 147472 | tf_op jit(solution)/shard_map/reduce_scatter | solution.py:252
  765.0 65.4 %reduce-scatter.18.cloned.1.call-done = bf16[144,512]{1,0:T(8,128)(2,1)} async-done(((bf16[1152,512]{1,0:T(8,128)(2,1)}), bf16[144,512]{1,0:T(8,128)(2,1)}) %reduce-scatter.18.cloned.1.call-update) | async-done | bytes 147472 | tf_op jit(solution)/shard_map/reduce_scatter | solution.py:270
  832.1 88.7 %reduce-scatter.26.cloned.1.call-done = bf16[144,1728]{1,0:T(8,128)(2,1)} async-done(((bf16[1152,1728]{1,0:T(8,128)(2,1)}), bf16[144,1728]{1,0:T(8,128)(2,1)}) %reduce-scatter.26.cloned.1.call-update) | async-done | bytes 497680
  923.1 88.9 %reduce-scatter.28.cloned.1.call-done = bf16[144,1728]{1,0:T(8,128)(2,1)} async-done(((bf16[1152,1728]{1,0:T(8,128)(2,1)}), bf16[144,1728]{1,0:T(8,128)(2,1)}) %reduce-scatter.28.cloned.1.call-update) | async-done | bytes 497680
  1019.2 83.7 %reduce-scatter.20.cloned.1.call-done = bf16[144,1728]{1,0:T(8,128)(2,1)} async-done(((bf16[1152,1728]{1,0:T(8,128)(2,1)}), bf16[144,1728]{1,0:T(8,128)(2,1)}) %reduce-scatter.20.cloned.1.call-update) | async-done | bytes 497680 | tf_op jit(solution)/shard_map/reduce_scatter | solution.py:185
  (295 shorter events, 99.6 us)
Async XLA Ops:
  7.2 91.9 %all-gather.6.cloned.1.call-start = ((), (), s32[]{:S(2)}) async-start(), calls=%async_computation.7 | async-start | bytes 1327104 | tf_op jit(solution)/shard_map/all_gather | solution.py:75
  7.9 174.4 %all-reduce.13.cloned.1.call-start = ((), (), s32[]{:S(2)}) async-start(), calls=%async_computation.8 | async-start | bytes 2359296 | tf_op jit(solution)/shard_map/psum | solution.py:136
  8.7 129.6 %collective-permute-start.1 = (s32[2,512]{1,0:T(2,128)S(1)}, s32[2,512]{1,0:T(2,128)S(1)}, u32[]{:S(2)}, u32[]{:S(2)}) collective-permute-start(s32[2,512]{1,0:T(2,128)S(1)} %pad_add_fusion.2), channel_id=1, source_target_pairs={{0,4},{4,8},{8,12},{1,5},{5,9},{9,13},{2,6},{6,10},{10,14},{3,7},{... | collective-permute-start | bytes 12296 | tf_op jit(solution)/shard_map/ppermute | solution.py:14
  14.3 87.4 %copy-start.37 = (f32[512]{0:T(512)}, f32[512]{0:T(512)S(1)}, u32[]{:S(2)}) copy-start(f32[512]{0:T(512)S(1)} %convert_element_type.178) | copy-start | bytes 6148
  60.5 41.2 %copy-start.73 = (f32[128]{0:T(128)}, f32[128]{0:T(128)S(1)}, u32[]{:S(2)}) copy-start(f32[128]{0:T(128)S(1)} %multiply_power_fusion) | copy-start | bytes 1540
  61.1 38.0 %copy-start.44 = (f32[1152]{0:T(1024)}, f32[1152]{0:T(1024)S(1)}, u32[]{:S(2)}) copy-start(f32[1152]{0:T(1024)S(1)} %get-tuple-element.146) | copy-start | bytes 13828
  62.7 36.3 %copy-start.52 = (f32[512]{0:T(512)}, f32[512]{0:T(512)S(1)}, u32[]{:S(2)}) copy-start(f32[512]{0:T(512)S(1)} %fusion.30) | copy-start | bytes 6148
  62.7 36.4 %copy-start.70 = (f32[512]{0:T(512)}, f32[512]{0:T(512)S(1)}, u32[]{:S(2)}) copy-start(f32[512]{0:T(512)S(1)} %fusion.116) | copy-start | bytes 6148
  62.7 36.3 %copy-start.63 = (f32[1,256]{1,0:T(1,128)}, f32[1,256]{1,0:T(1,128)S(1)}, u32[]{:S(2)}) copy-start(f32[1,256]{1,0:T(1,128)S(1)} %get-tuple-element.171) | copy-start | bytes 3076
  62.8 38.8 %copy-start.61 = (f32[1,256]{1,0:T(1,128)}, f32[1,256]{1,0:T(1,128)S(1)}, u32[]{:S(2)}) copy-start(f32[1,256]{1,0:T(1,128)S(1)} %get-tuple-element.172) | copy-start | bytes 3076
  62.8 36.3 %copy-start.1 = (bf16[1,512,1152]{2,1,0:T(8,128)(2,1)S(1)}, bf16[1,512,1152]{2,1,0:T(8,128)(2,1)}, u32[]{:S(2)}) copy-start(bf16[1,512,1152]{2,1,0:T(8,128)(2,1)} %param.15) | copy-start | bytes 3538948
  101.5 36.7 %copy-start.60 = (s32[1,512]{1,0:T(1,128)S(1)}, s32[1,512]{1,0:T(1,128)}, u32[]{:S(2)}) copy-start(s32[1,512]{1,0:T(1,128)} %param.16) | copy-start | bytes 6148
  101.6 36.7 %copy-start.67 = (s32[1,512]{1,0:T(1,128)S(1)}, s32[1,512]{1,0:T(1,128)}, u32[]{:S(2)}) copy-start(s32[1,512]{1,0:T(1,128)} %param.17) | copy-start | bytes 6148
  103.0 35.3 %collective-permute-start = (bf16[512,512]{0,1:T(8,128)(2,1)S(1)}, bf16[512,512]{0,1:T(8,128)(2,1)S(1)}, u32[]{:S(2)}, u32[]{:S(2)}) collective-permute-start(bf16[512,512]{0,1:T(8,128)(2,1)S(1)} %pad_maximum_fusion.2), channel_id=1, source_target_pairs={{0,4},{4,8},{8,12},{1,5},{5,9},{9,13},{2,6},{6,10},{10,14},{3,7},{... | collective-permute-start | bytes 1572872 | tf_op jit(solution)/shard_map/ppermute | solution.py:14
  143.0 165.0 %all-gather.8.cloned.1.call-start = ((), (), s32[]{:S(2)}) async-start(), calls=%async_computation.9 | async-start | bytes 9289728 | tf_op jit(solution)/shard_map/all_gather | solution.py:147
  145.4 234.7 %all-gather.10.cloned.1.call-start = ((), (), s32[]{:S(2)}) async-start(), calls=%async_computation.10 | async-start | bytes 4644864 | tf_op jit(solution)/shard_map/all_gather | solution.py:154
  145.9 276.7 %all-reduce.15.cloned.1.call-start = ((), (), s32[]{:S(2)}) async-start(), calls=%async_computation.11 | async-start | bytes 2359296 | tf_op jit(solution)/shard_map/psum | solution.py:152
  182.3 125.7 %copy-start = (bf16[512,1152]{1,0:T(8,128)(2,1)S(1)}, bf16[512,1152]{1,0:T(8,128)(2,1)}, u32[]{:S(2)}) copy-start(bf16[512,1152]{1,0:T(8,128)(2,1)} %all-reduce.13.cloned.1.call-done) | copy-start | bytes 3538948
  386.4 100.0 %all-reduce.17.cloned.1.call-start = ((), (), s32[]{:S(2)}) async-start(), calls=%async_computation.12 | async-start | bytes 2359296 | tf_op jit(solution)/shard_map/psum | solution.py:176
  448.5 114.3 %all-reduce.19.cloned.1.call-start = ((), (), s32[]{:S(2)}) async-start(), calls=%async_computation.20 | async-start | bytes 3407872 | tf_op jit(solution)/shard_map/psum | solution.py:237
  501.8 15.5 %collective-permute-start.2 = (bf16[512,512]{0,1:T(8,128)(2,1)S(1)}, bf16[512,512]{0,1:T(8,128)(2,1)S(1)}, u32[]{:S(2)}, u32[]{:S(2)}) collective-permute-start(bf16[512,512]{0,1:T(8,128)(2,1)S(1)} %fusion.66), channel_id=1, source_target_pairs={{4,0},{8,4},{12,8},{5,1},{9,5},{13,9},{6,2},{10,6},{14,10},{7,3},{... | collective-permute-start | bytes 1572872 | tf_op jit(solution)/shard_map/ppermute | solution.py:14
  518.3 115.9 %reduce-scatter.24.cloned.1.call-start = ((), (), s32[]{:S(2)}) async-start(), calls=%async_computation.17 | async-start | bytes 73728
  533.0 31.0 %copy-start.75 = (f32[128]{0:T(128)S(1)}, f32[128]{0:T(128)}, u32[]{:S(2)}) copy-start(f32[128]{0:T(128)} %copy-done.73) | copy-start | bytes 1540
  533.0 32.2 %copy-start.10 = (f32[512,512]{0,1:T(8,128)S(1)}, f32[512,512]{0,1:T(8,128)}, u32[]{:S(2)}) copy-start(f32[512,512]{0,1:T(8,128)} %copy-done.9) | copy-start | bytes 3145732
  533.0 32.2 %copy-start.41 = (f32[512]{0:T(512)S(1)}, f32[512]{0:T(512)}, u32[]{:S(2)}) copy-start(f32[512]{0:T(512)} %copy-done.40) | copy-start | bytes 6148
  533.0 32.2 %copy-start.62 = (f32[1,256]{1,0:T(1,128)S(1)}, f32[1,256]{1,0:T(1,128)}, u32[]{:S(2)}) copy-start(f32[1,256]{1,0:T(1,128)} %copy-done.61) | copy-start | bytes 3076
  571.6 124.7 %reduce-scatter.22.cloned.1.call-start = ((), (), s32[]{:S(2)}) async-start(), calls=%async_computation.16 | async-start | bytes 331776
  574.6 188.8 %reduce-scatter.16.cloned.1.call-start = ((), (), s32[]{:S(2)}) async-start(), calls=%async_computation.13 | async-start | bytes 1327104 | tf_op jit(solution)/shard_map/reduce_scatter | solution.py:252
  575.9 254.5 %reduce-scatter.18.cloned.1.call-start = ((), (), s32[]{:S(2)}) async-start(), calls=%async_computation.14 | async-start | bytes 1327104 | tf_op jit(solution)/shard_map/reduce_scatter | solution.py:270
  579.2 341.6 %reduce-scatter.26.cloned.1.call-start = ((), (), s32[]{:S(2)}) async-start(), calls=%async_computation.18 | async-start | bytes 4644864
  598.6 413.3 %reduce-scatter.28.cloned.1.call-start = ((), (), s32[]{:S(2)}) async-start(), calls=%async_computation.19 | async-start | bytes 4644864
  605.2 497.7 %reduce-scatter.20.cloned.1.call-start = ((), (), s32[]{:S(2)}) async-start(), calls=%async_computation.15 | async-start | bytes 4644864 | tf_op jit(solution)/shard_map/reduce_scatter | solution.py:185
  (70 other events, 327.8 us)
Sparse Core Ops, SparseCore 0:
  10.1 43.7 all-gather.5
  143.1 39.0 all-reduce.12
  185.0 122.9 all-gather.7
  310.0 70.0 all-gather.9
  386.5 36.1 all-reduce.14
  448.6 37.7 all-reduce.16
  518.4 44.2 all-reduce.18
  571.7 62.4 reduce-scatter.23
  638.1 58.1 reduce-scatter.21
  699.5 63.8 reduce-scatter.15
  766.8 63.5 reduce-scatter.17
  833.8 86.9 reduce-scatter.25
  924.4 87.5 reduce-scatter.27
  1015.3 87.5 reduce-scatter.19
where the time goes:
time: 1120 us; the launch traced here: 1110 us
  waiting for transfers between devices  796 us (71%)
  blocking collectives  120 us (11%)
  matrix products  72.4 us (6%)
  local copies, waits for them, and re-layouts  50.5 us (5%)
  other arithmetic  49.1 us (4%)
  between operations  15.3 us (1%)
    unnamed x18, waiting for transfers between devices  256 us
    all_gather x1, waiting for transfers between devices, shards(): lax.all_gather(w_gateup, ('fsdp', 'context'), axis=0, tiled=True)  119 us
    reduce_scatter x1, waiting for transfers between devices, shards(): lax.psum_scatter(part.astype(jnp.bfloat16), ('fsdp', 'context'), scatter_...  83.7 us
    reduce_scatter x1, waiting for transfers between devices, shards(): lax.psum_scatter(jnp.stack([contract_first(features, d_query_low), contra...  65.6 us
    reduce_scatter x1, waiting for transfers between devices, shards(): lax.psum_scatter(keyval_term.astype(jnp.bfloat16), ('fsdp', 'context'), s...  65.4 us
    all_gather x1, waiting for transfers between devices, shards(): lax.all_gather(w_down, ('fsdp', 'context'), axis=0, tiled=True)  58.5 us
    unnamed x180, local copies, waits for them, and re-layouts  39.6 us
    psum x1, waiting for transfers between devices, shards(): lax.psum(d_normed_part.astype(jnp.bfloat16), 'tensor').astype(jnp.float32)  36.1 us
  transfers between devices with their start and end apart: 17, of which 14 were waited for; matrix products, arithmetic and copies ran while one was open for 9% of the time, Pallas kernels for 0%

commit v1 on v0

--- a/solution.py
+++ b/solution.py
@@ -133,9 +133,9 @@
 
     mixed_blocks, log_blocks = lax.map(forward_block, block_starts)
     mixed_low = mixed_blocks.reshape(tokens, local_heads * HD)
-    branch = lax.psum(contract_last(mixed_low, out_all).astype(jnp.bfloat16), "tensor").astype(
-        jnp.float32
-    )
+    branch = jnp.sum(
+        lax.all_gather(contract_last(mixed_low, out_all).astype(jnp.bfloat16), "tensor"), axis=0
+    ).astype(jnp.float32)
     post_attn, post_attn_back = jax.vjp(rms_norm, branch, gains_f[1])
     hidden = inputs + post_attn
     normed_mlp_f, pre_mlp_back = jax.vjp(rms_norm, hidden, gains_f[2])

time: 1120 us -> 1120 us (level)
    psum x1 -> x0, waiting for transfers between devices: 36.1 us -> none  [shards(): lax.psum(contract_last(mixed_low, out_all).astype(jnp.bfloat16), 'tensor')]
    all_gather x0 -> x1, waiting for transfers between devices: none -> 35.9 us  [shards(): lax.all_gather(contract_last(mixed_low, out_all).astype(jnp.bfloat16), 't...]
    unnamed x180 -> x178, local copies, waits for them, and re-layouts: 39.6 us -> 39.6 us
where the time goes in v1:
time: 1120 us; the launch traced here: 1110 us
  waiting for transfers between devices  793 us (71%)
  blocking collectives  120 us (11%)
  matrix products  72.5 us (6%)
  other arithmetic  51.1 us (5%)
  local copies, waits for them, and re-layouts  50.4 us (4%)
  between operations  15.3 us (1%)
    unnamed x18, waiting for transfers between devices  256 us
    all_gather x1, waiting for transfers between devices, shards(): lax.all_gather(w_gateup, ('fsdp', 'context'), axis=0, tiled=True)  117 us
    reduce_scatter x1, waiting for transfers between devices, shards(): lax.psum_scatter(part.astype(jnp.bfloat16), ('fsdp', 'context'), scatter_...  83.7 us
    reduce_scatter x1, waiting for transfers between devices, shards(): lax.psum_scatter(jnp.stack([contract_first(features, d_query_low), contra...  65.4 us
    reduce_scatter x1, waiting for transfers between devices, shards(): lax.psum_scatter(keyval_term.astype(jnp.bfloat16), ('fsdp', 'context'), s...  65.4 us
    all_gather x1, waiting for transfers between devices, shards(): lax.all_gather(w_down, ('fsdp', 'context'), axis=0, tiled=True)  58.5 us
    unnamed x178, local copies, waits for them, and re-layouts  39.6 us
    psum x1, waiting for transfers between devices, shards(): lax.psum(d_normed_part.astype(jnp.bfloat16), 'tensor').astype(jnp.float32)  36.1 us
  transfers between devices with their start and end apart: 17, of which 14 were waited for; matrix products, arithmetic and copies ran while one was open for 9% of the time, Pallas kernels for 0%

profile of v1, /device:TPU:0, one launch (start us, length us, event | category | flops | bytes accessed | tf_op | source)
XLA Modules:
  0.0 1111.3 jit_solution(3614129570835466476)
XLA Ops:
  8.7 4.9 collective-permute-start.1
  14.3 18.8 %all-gather.2 = bf16[8,32,2]{1,2,0:T(2,128)(2,1)S(1)} all-gather(bf16[1,32,2]{1,2,0:T(2,128)(2,1)} %bitcast.268), channel_id=1, replica_groups=mesh['fsdp'=2,'context'=4,'tensor'=4] {'fsdp','context'}, dimensions={0}, use_global_device_ids=true | all-gather | bytes 1152 | tf_op jit(solution)/shard_map/all_gather | solution.py:73
  33.2 27.2 %all-gather.1 = bf16[8,144,4]{1,2,0:T(4,128)(2,1)S(1)} all-gather(bf16[1,144,4]{1,2,0:T(4,128)(2,1)} %bitcast.267), channel_id=1, replica_groups=mesh['fsdp'=2,'context'=4,'tensor'=4] {'fsdp','context'}, dimensions={0}, use_global_device_ids=true | all-gather | bytes 10368 | tf_op jit(solution)/shard_map/all_gather | solution.py:72
  62.8 32.5 %all_gather.32 = bf16[1152,256]{1,0:T(8,128)(2,1)S(1)} all-gather(bf16[144,256]{1,0:T(8,128)(2,1)} %param.20), channel_id=1, replica_groups=mesh['fsdp'=2,'context'=4,'tensor'=4] {'fsdp','context'}, dimensions={0}, use_global_device_ids=true | all-gather | bytes 663552 | tf_op jit(solution)/shard_map/all_gather | solution.py:74
  104.4 33.8 %all_gather.33 = bf16[1152,256]{1,0:T(8,128)(2,1)S(1)} all-gather(bf16[144,256]{1,0:T(8,128)(2,1)S(1)} %copy-done.31), channel_id=1, replica_groups=mesh['fsdp'=2,'context'=4,'tensor'=4] {'fsdp','context'}, dimensions={0}, use_global_device_ids=true | all-gather | bytes 663552 | tf_op jit(solution)/shard_map/all_gather | solution.py:76
  146.2 35.9 %all-gather.14.cloned.1.call-done = bf16[2048,1152]{1,0:T(8,128)(2,1)} async-done(((bf16[512,1152]{1,0:T(8,128)(2,1)}), bf16[2048,1152]{1,0:T(8,128)(2,1)}) %all-gather.14.cloned.1.call-update) | async-done | bytes 4718608 | tf_op jit(solution)/shard_map/all_gather | solution.py:137
  182.1 3.7 reduce_sum.200
  190.5 117.2 %all-gather.10.cloned.1.call-done = bf16[1152,2,1728]{2,0,1:T(8,128)(2,1)} async-done(((bf16[144,2,1728]{2,0,1:T(8,128)(2,1)}), bf16[1152,2,1728]{2,0,1:T(8,128)(2,1)}) %all-gather.10.cloned.1.call-update) | async-done | bytes 7962640 | tf_op jit(solution)/shard_map/all_gather | solution.py:147
  307.7 8.2 fusion.114
  321.2 58.5 %all-gather.12.cloned.1.call-done = bf16[1152,1728]{1,0:T(8,128)(2,1)} async-done(((bf16[144,1728]{1,0:T(8,128)(2,1)}), bf16[1152,1728]{1,0:T(8,128)(2,1)}) %all-gather.12.cloned.1.call-update) | async-done | bytes 3981328 | tf_op jit(solution)/shard_map/all_gather | solution.py:154
  379.8 6.3 convolution_convert_fusion.4
  386.4 36.0 %all-reduce.12.cloned.1.call-done = bf16[512,1152]{1,0:T(8,128)(2,1)} async-done(((bf16[512,1152]{1,0:T(8,128)(2,1)}), bf16[512,1152]{1,0:T(8,128)(2,1)}) %all-reduce.12.cloned.1.call-update) | async-done | bytes 1179664 | tf_op jit(solution)/shard_map/psum | solution.py:152
  427.6 10.7 multiply_bitcast_fusion
  440.0 8.1 fusion.7
  449.9 36.1 %all-reduce.14.cloned.1.call-done = bf16[512,1152]{1,0:T(8,128)(2,1)} async-done(((bf16[512,1152]{1,0:T(8,128)(2,1)}), bf16[512,1152]{1,0:T(8,128)(2,1)}) %all-reduce.14.cloned.1.call-update) | async-done | bytes 1179664 | tf_op jit(solution)/shard_map/psum | solution.py:176
  486.1 3.6 fusion.29
  489.8 5.1 fusion.25
  505.4 11.6 %collective-permute-done.2 = bf16[512,512]{0,1:T(8,128)(2,1)S(1)} collective-permute-done((bf16[512,512]{0,1:T(8,128)(2,1)S(1)}, bf16[512,512]{0,1:T(8,128)(2,1)S(1)}, u32[]{:S(2)}, u32[]{:S(2)}) %collective-permute-start.2) | collective-permute-done | bytes 524320 | tf_op jit(solution)/shard_map/ppermute | solution.py:14
  523.2 7.2 psum.39
  535.3 27.2 %all-reduce.16.cloned.1.call-done = (bf16[512,1152]{1,0:T(8,128)(2,1)}, bf16[512,512]{0,1:T(8,128)(2,1)}) async-done(((bf16[512,1152]{1,0:T(8,128)(2,1)}, bf16[512,512]{0,1:T(8,128)(2,1)}), (bf16[512,1152]{1,0:T(8,128)(2,1)}, bf16[512,512]{0,1:T(8,128)(2,1)})) %all-reduce.16.cloned.1.call-update) | async-done | bytes 1703952 | tf_op jit(solution)/shard_map/psum | solution.py:237
  579.1 9.3 convolution_convert_fusion
  591.9 6.4 copy.38
  598.4 6.5 copy.40
  606.5 6.3 convolution_convert_fusion.1
  613.5 4.0 fusion.52
  617.5 16.4 %reduce-scatter.24.cloned.1.call-done = bf16[32,2]{1,0:T(8,128)(2,1)} async-done(((bf16[256,2]{1,0:T(8,128)(2,1)}), bf16[32,2]{1,0:T(8,128)(2,1)}) %reduce-scatter.24.cloned.1.call-update) | async-done | bytes 144
  635.3 60.7 %reduce-scatter.22.cloned.1.call-done = bf16[144,4]{1,0:T(8,128)(2,1)} async-done(((bf16[1152,4]{1,0:T(8,128)(2,1)}), bf16[144,4]{1,0:T(8,128)(2,1)}) %reduce-scatter.22.cloned.1.call-update) | async-done | bytes 1168
  697.5 65.4 %reduce-scatter.16.cloned.1.call-done = bf16[144,2,256]{2,0,1:T(8,128)(2,1)} async-done(((bf16[1152,2,256]{2,0,1:T(8,128)(2,1)}), bf16[144,2,256]{2,0,1:T(8,128)(2,1)}) %reduce-scatter.16.cloned.1.call-update) | async-done | bytes 147472 | tf_op jit(solution)/shard_map/reduce_scatter | solution.py:252
  764.6 65.4 %reduce-scatter.18.cloned.1.call-done = bf16[144,512]{1,0:T(8,128)(2,1)} async-done(((bf16[1152,512]{1,0:T(8,128)(2,1)}), bf16[144,512]{1,0:T(8,128)(2,1)}) %reduce-scatter.18.cloned.1.call-update) | async-done | bytes 147472 | tf_op jit(solution)/shard_map/reduce_scatter | solution.py:270
  831.6 88.8 %reduce-scatter.26.cloned.1.call-done = bf16[144,1728]{1,0:T(8,128)(2,1)} async-done(((bf16[1152,1728]{1,0:T(8,128)(2,1)}), bf16[144,1728]{1,0:T(8,128)(2,1)}) %reduce-scatter.26.cloned.1.call-update) | async-done | bytes 497680
  922.6 88.9 %reduce-scatter.28.cloned.1.call-done = bf16[144,1728]{1,0:T(8,128)(2,1)} async-done(((bf16[1152,1728]{1,0:T(8,128)(2,1)}), bf16[144,1728]{1,0:T(8,128)(2,1)}) %reduce-scatter.28.cloned.1.call-update) | async-done | bytes 497680
  1018.8 83.7 %reduce-scatter.20.cloned.1.call-done = bf16[144,1728]{1,0:T(8,128)(2,1)} async-done(((bf16[1152,1728]{1,0:T(8,128)(2,1)}), bf16[144,1728]{1,0:T(8,128)(2,1)}) %reduce-scatter.20.cloned.1.call-update) | async-done | bytes 497680 | tf_op jit(solution)/shard_map/reduce_scatter | solution.py:185
  (294 shorter events, 101.4 us)
Async XLA Ops:
  7.2 91.9 %all-gather.8.cloned.1.call-start = ((), (), s32[]{:S(2)}) async-start(), calls=%async_computation.7 | async-start | bytes 1327104 | tf_op jit(solution)/shard_map/all_gather | solution.py:75
  7.9 174.2 %all-gather.14.cloned.1.call-start = ((), (), s32[]{:S(2)}) async-start(), calls=%async_computation.15 | async-start | bytes 5898240 | tf_op jit(solution)/shard_map/all_gather | solution.py:137
  8.7 129.6 %collective-permute-start.1 = (s32[2,512]{1,0:T(2,128)S(1)}, s32[2,512]{1,0:T(2,128)S(1)}, u32[]{:S(2)}, u32[]{:S(2)}) collective-permute-start(s32[2,512]{1,0:T(2,128)S(1)} %pad_add_fusion.2), channel_id=1, source_target_pairs={{0,4},{4,8},{8,12},{1,5},{5,9},{9,13},{2,6},{6,10},{10,14},{3,7},{... | collective-permute-start | bytes 12296 | tf_op jit(solution)/shard_map/ppermute | solution.py:14
  14.3 87.4 %copy-start.36 = (f32[512]{0:T(512)}, f32[512]{0:T(512)S(1)}, u32[]{:S(2)}) copy-start(f32[512]{0:T(512)S(1)} %convert_element_type.180) | copy-start | bytes 6148
  60.5 41.2 %copy-start.72 = (f32[128]{0:T(128)}, f32[128]{0:T(128)S(1)}, u32[]{:S(2)}) copy-start(f32[128]{0:T(128)S(1)} %multiply_power_fusion) | copy-start | bytes 1540
  61.1 38.0 %copy-start.43 = (f32[1152]{0:T(1024)}, f32[1152]{0:T(1024)S(1)}, u32[]{:S(2)}) copy-start(f32[1152]{0:T(1024)S(1)} %get-tuple-element.146) | copy-start | bytes 13828
  62.7 36.3 %copy-start.51 = (f32[512]{0:T(512)}, f32[512]{0:T(512)S(1)}, u32[]{:S(2)}) copy-start(f32[512]{0:T(512)S(1)} %fusion.30) | copy-start | bytes 6148
  62.7 36.4 %copy-start.69 = (f32[512]{0:T(512)}, f32[512]{0:T(512)S(1)}, u32[]{:S(2)}) copy-start(f32[512]{0:T(512)S(1)} %fusion.116) | copy-start | bytes 6148
  62.7 36.3 %copy-start.62 = (f32[1,256]{1,0:T(1,128)}, f32[1,256]{1,0:T(1,128)S(1)}, u32[]{:S(2)}) copy-start(f32[1,256]{1,0:T(1,128)S(1)} %get-tuple-element.171) | copy-start | bytes 3076
  62.8 38.8 %copy-start.60 = (f32[1,256]{1,0:T(1,128)}, f32[1,256]{1,0:T(1,128)S(1)}, u32[]{:S(2)}) copy-start(f32[1,256]{1,0:T(1,128)S(1)} %get-tuple-element.172) | copy-start | bytes 3076
  62.8 36.3 %copy-start = (bf16[1,512,1152]{2,1,0:T(8,128)(2,1)S(1)}, bf16[1,512,1152]{2,1,0:T(8,128)(2,1)}, u32[]{:S(2)}) copy-start(bf16[1,512,1152]{2,1,0:T(8,128)(2,1)} %param.15) | copy-start | bytes 3538948
  101.6 36.7 %copy-start.59 = (s32[1,512]{1,0:T(1,128)S(1)}, s32[1,512]{1,0:T(1,128)}, u32[]{:S(2)}) copy-start(s32[1,512]{1,0:T(1,128)} %param.16) | copy-start | bytes 6148
  101.6 36.7 %copy-start.66 = (s32[1,512]{1,0:T(1,128)S(1)}, s32[1,512]{1,0:T(1,128)}, u32[]{:S(2)}) copy-start(s32[1,512]{1,0:T(1,128)} %param.17) | copy-start | bytes 6148
  103.1 35.3 %collective-permute-start = (bf16[512,512]{0,1:T(8,128)(2,1)S(1)}, bf16[512,512]{0,1:T(8,128)(2,1)S(1)}, u32[]{:S(2)}, u32[]{:S(2)}) collective-permute-start(bf16[512,512]{0,1:T(8,128)(2,1)S(1)} %pad_maximum_fusion.2), channel_id=1, source_target_pairs={{0,4},{4,8},{8,12},{1,5},{5,9},{9,13},{2,6},{6,10},{10,14},{3,7},{... | collective-permute-start | bytes 1572872 | tf_op jit(solution)/shard_map/ppermute | solution.py:14
  143.0 164.7 %all-gather.10.cloned.1.call-start = ((), (), s32[]{:S(2)}) async-start(), calls=%async_computation.8 | async-start | bytes 9289728 | tf_op jit(solution)/shard_map/all_gather | solution.py:147
  145.4 234.4 %all-gather.12.cloned.1.call-start = ((), (), s32[]{:S(2)}) async-start(), calls=%async_computation.9 | async-start | bytes 4644864 | tf_op jit(solution)/shard_map/all_gather | solution.py:154
  146.0 276.4 %all-reduce.12.cloned.1.call-start = ((), (), s32[]{:S(2)}) async-start(), calls=%async_computation.10 | async-start | bytes 2359296 | tf_op jit(solution)/shard_map/psum | solution.py:152
  386.1 100.0 %all-reduce.14.cloned.1.call-start = ((), (), s32[]{:S(2)}) async-start(), calls=%async_computation.11 | async-start | bytes 2359296 | tf_op jit(solution)/shard_map/psum | solution.py:176
  448.2 114.3 %all-reduce.16.cloned.1.call-start = ((), (), s32[]{:S(2)}) async-start(), calls=%async_computation.20 | async-start | bytes 3407872 | tf_op jit(solution)/shard_map/psum | solution.py:237
  501.5 15.5 %collective-permute-start.2 = (bf16[512,512]{0,1:T(8,128)(2,1)S(1)}, bf16[512,512]{0,1:T(8,128)(2,1)S(1)}, u32[]{:S(2)}, u32[]{:S(2)}) collective-permute-start(bf16[512,512]{0,1:T(8,128)(2,1)S(1)} %fusion.66), channel_id=1, source_target_pairs={{4,0},{8,4},{12,8},{5,1},{9,5},{13,9},{6,2},{10,6},{14,10},{7,3},{... | collective-permute-start | bytes 1572872 | tf_op jit(solution)/shard_map/ppermute | solution.py:14
  518.0 115.9 %reduce-scatter.24.cloned.1.call-start = ((), (), s32[]{:S(2)}) async-start(), calls=%async_computation.17 | async-start | bytes 73728
  532.7 31.0 %copy-start.38 = (f32[512]{0:T(512)S(1)}, f32[512]{0:T(512)}, u32[]{:S(2)}) copy-start(f32[512]{0:T(512)} %copy-done.36) | copy-start | bytes 6148
  532.7 31.0 %copy-start.74 = (f32[128]{0:T(128)S(1)}, f32[128]{0:T(128)}, u32[]{:S(2)}) copy-start(f32[128]{0:T(128)} %copy-done.72) | copy-start | bytes 1540
  532.7 32.2 %copy-start.9 = (f32[512,512]{0,1:T(8,128)S(1)}, f32[512,512]{0,1:T(8,128)}, u32[]{:S(2)}) copy-start(f32[512,512]{0,1:T(8,128)} %copy-done.8) | copy-start | bytes 3145732
  532.7 32.2 %copy-start.40 = (f32[512]{0:T(512)S(1)}, f32[512]{0:T(512)}, u32[]{:S(2)}) copy-start(f32[512]{0:T(512)} %copy-done.39) | copy-start | bytes 6148
  532.7 32.2 %copy-start.61 = (f32[1,256]{1,0:T(1,128)S(1)}, f32[1,256]{1,0:T(1,128)}, u32[]{:S(2)}) copy-start(f32[1,256]{1,0:T(1,128)} %copy-done.60) | copy-start | bytes 3076
  571.3 124.7 %reduce-scatter.22.cloned.1.call-start = ((), (), s32[]{:S(2)}) async-start(), calls=%async_computation.16 | async-start | bytes 331776
  574.3 188.6 %reduce-scatter.16.cloned.1.call-start = ((), (), s32[]{:S(2)}) async-start(), calls=%async_computation.12 | async-start | bytes 1327104 | tf_op jit(solution)/shard_map/reduce_scatter | solution.py:252
  575.6 254.3 %reduce-scatter.18.cloned.1.call-start = ((), (), s32[]{:S(2)}) async-start(), calls=%async_computation.13 | async-start | bytes 1327104 | tf_op jit(solution)/shard_map/reduce_scatter | solution.py:270
  579.0 341.4 %reduce-scatter.26.cloned.1.call-start = ((), (), s32[]{:S(2)}) async-start(), calls=%async_computation.18 | async-start | bytes 4644864
  598.3 413.2 %reduce-scatter.28.cloned.1.call-start = ((), (), s32[]{:S(2)}) async-start(), calls=%async_computation.19 | async-start | bytes 4644864
  604.9 497.6 %reduce-scatter.20.cloned.1.call-start = ((), (), s32[]{:S(2)}) async-start(), calls=%async_computation.14 | async-start | bytes 4644864 | tf_op jit(solution)/shard_map/reduce_scatter | solution.py:185
  (69 other events, 296.9 us)
Sparse Core Ops, SparseCore 0:
  10.1 43.7 all-gather.7
  143.1 38.9 all-gather.13
  184.9 122.8 all-gather.9
  309.7 70.0 all-gather.11
  386.2 36.1 all-reduce.11
  448.3 37.7 all-reduce.13
  518.2 44.2 all-reduce.15
  571.4 62.4 reduce-scatter.23
  637.8 58.1 reduce-scatter.21
  699.3 63.6 reduce-scatter.15
  766.3 63.5 reduce-scatter.17
  833.4 86.9 reduce-scatter.25
  923.9 87.5 reduce-scatter.27
  1014.9 87.5 reduce-scatter.19
